TPU v7x, 256 devices: a whole 4x4x8 slice. The times are simulated.
256 devices in a mesh: patch: 32 (over y, z_hi, core), chan: 8 (over z_lo, x).
Axes of the slice: x: 4, y: 4, z: 8 (z_hi: 4, z_lo: 2; z = z_hi * 2 + z_lo), core: 2. Of those that a mesh axis runs over, the one named last changes fastest.
Arguments:
- tokens: bfloat16 [1, 16384, 1280], P(None, 'patch'), may hold values from -12 to 12
- stale_k: bfloat16 [1, 16384, 1024], P(None, 'patch', 'chan'), may hold values from -64 to 64
- stale_v: bfloat16 [1, 16384, 1024], P(None, 'patch', 'chan'), may hold values from -6 to 6
- w_query: bfloat16 [1280, 1024], P(None, 'chan'), may hold values from -0.15625 to 0.15625
- w_key: bfloat16 [1280, 1024], P(None, 'chan'), may hold values from -0.4375 to 0.4375
- w_value: bfloat16 [1280, 1024], P(None, 'chan'), may hold values from -0.15625 to 0.15625
- w_out: bfloat16 [1024, 1280], P('chan'), may hold values from -0.1875 to 0.1875
- ff_value: bfloat16 [1280, 5120], P(None, 'chan'), may hold values from -0.15625 to 0.15625
- ff_gate: bfloat16 [1280, 5120], P(None, 'chan'), may hold values from -0.15625 to 0.15625
- ff_down: bfloat16 [5120, 1280], P('chan'), may hold values from -0.078125 to 0.078125
Outputs:
- layer_out: bfloat16 [1, 16384, 1280], P(None, 'patch', 'chan')
All inputs are finite; a program needn't handle non-finite values.
Results may differ from a plain program's by a relative error of at most 0.0095.
Values may be sent and summed in bfloat16 or wider, within the bound.
A program may use at most 64 MiB of HBM per device.

v0:
```python
import jax
import jax.numpy as jnp
from jax import lax
from jax.sharding import PartitionSpec as P

HD = 64


def in_one_piece(arrays, axis, dim, along):
    both = jnp.concatenate(arrays, axis=along)
    result, at, done = (lax.all_gather(both, axis, axis=dim, tiled=True), 0, [])
    for a in arrays:
        done.append(lax.slice_in_dim(result, at, at + a.shape[along], axis=along))
        at += a.shape[along]
    return tuple(done)


def split_up(shard, dim, devices):
    before, after = (shard.shape[:dim], shard.shape[dim + 1 :])
    return jnp.moveaxis(shard.reshape(*before, devices, -1, *after), dim, 0)


def sent_and_summed(shard, axis, dim):
    devices = lax.axis_size(axis)
    pieces = lax.all_to_all(split_up(shard, dim, devices), axis, 0, 0, tiled=True)
    return jnp.sum(pieces.astype(jnp.float32), axis=0)


def in_order(pieces, dim):
    lengths = list(pieces.shape[1:])
    lengths[dim] *= pieces.shape[0]
    return jnp.moveaxis(pieces, 0, dim).reshape(lengths)


def from_everyone(shard, axis):
    copies = jnp.broadcast_to(shard, (lax.axis_size(axis), *shard.shape))
    return lax.all_to_all(copies, axis, split_axis=0, concat_axis=0, tiled=True)


def collect(shard, axis, dim):
    return in_order(from_everyone(shard, axis), dim)


def layer_norm(values):
    mean = jnp.mean(values, axis=-1, keepdims=True)
    centered = values - mean
    var = jnp.mean(centered * centered, axis=-1, keepdims=True)
    return centered * lax.rsqrt(var + 1e-05)


def project(inputs, weight):
    return jnp.einsum("btd,de->bte", inputs, weight, preferred_element_type=jnp.float32)


def per_device(
    tokens, stale_k, stale_v, w_query, w_key, w_value, w_out, ff_value, ff_gate, ff_down
):
    all_keys, all_values = in_one_piece((stale_k, stale_v), "patch", 1, 0)
    batch_size, row_count, width = tokens.shape
    head_count = w_query.shape[1] // HD
    patch_id = lax.axis_index("patch")
    score_scale = 1.0 / HD**0.5
    normed = layer_norm(tokens.astype(jnp.float32)).astype(jnp.bfloat16)
    queries = (
        project(normed, w_query).astype(jnp.bfloat16).reshape(batch_size, row_count, head_count, HD)
    )
    key_fresh = project(normed, w_key).astype(jnp.bfloat16)
    value_fresh = project(normed, w_value).astype(jnp.bfloat16)

    def attend(running, key_rows, value_rows, first_row):
        accum, running_max, totals = running
        block_rows = key_rows.shape[1]
        key_rows = key_rows.reshape(batch_size, block_rows, head_count, HD)
        value_rows = value_rows.reshape(batch_size, block_rows, head_count, HD)
        scores = (
            jnp.einsum("bqhd,bkhd->bhqk", queries, key_rows, preferred_element_type=jnp.float32)
            * score_scale
        )
        if first_row is not None:
            row_ids = first_row + jnp.arange(block_rows, dtype=jnp.int32)
            own_rows = row_ids // row_count == patch_id
            scores = jnp.where(own_rows[None, None, None, :], -1e30, scores)
        new_max = jnp.maximum(running_max, jnp.max(scores, axis=-1))
        weights = jnp.exp(scores - new_max[..., None])
        rescale = jnp.exp(running_max - new_max)
        totals = totals * rescale + jnp.sum(weights, axis=-1)
        accum = accum * rescale[..., None] + jnp.einsum(
            "bhqk,bkhd->bhqd",
            weights.astype(jnp.bfloat16),
            value_rows,
            preferred_element_type=jnp.float32,
        )
        return (accum, new_max, totals)

    start_state = (
        jnp.zeros((batch_size, head_count, row_count, HD), jnp.float32),
        jnp.full((batch_size, head_count, row_count), -1e30, jnp.float32),
        jnp.zeros((batch_size, head_count, row_count), jnp.float32),
    )
    running = attend(start_state, key_fresh, value_fresh, None)
    key_rows = all_keys
    value_rows = all_values
    piece_rows = key_rows.shape[1]

    def turn(block_id, acc):
        offset = block_id * 1024
        key_block = lax.dynamic_slice_in_dim(key_rows, offset, 1024, 1)
        value_block = lax.dynamic_slice_in_dim(value_rows, offset, 1024, 1)
        return attend(acc, key_block, value_block, offset)

    running = lax.fori_loop(0, piece_rows // 1024, turn, running)
    accum, running_max, totals = running
    attended = jnp.transpose(accum / totals[..., None], (0, 2, 1, 3))
    attended = attended.reshape(batch_size, row_count, head_count * HD).astype(jnp.bfloat16)
    partial_value = project(attended, w_out)
    chan_id = lax.axis_index("chan")
    share_width = width // lax.axis_size("chan")
    attn_part = sent_and_summed(partial_value.astype(jnp.bfloat16), "chan", 2)
    resid_share = (
        lax.dynamic_slice_in_dim(tokens, chan_id * share_width, share_width, 2).astype(jnp.float32)
        + attn_part
    )
    resid = collect(resid_share.astype(jnp.bfloat16), "chan", 2).astype(resid_share.dtype)
    normed_two = layer_norm(resid).astype(jnp.bfloat16)
    ff_val = project(normed_two, ff_value)
    gate_out = project(normed_two, ff_gate)
    gated = (ff_val * jax.nn.gelu(gate_out, approximate=False)).astype(jnp.bfloat16)
    down_out = project(gated, ff_down)
    ffn_part = sent_and_summed(down_out.astype(jnp.bfloat16), "chan", 2)
    return (resid_share + ffn_part).astype(jnp.bfloat16)


def solution(mesh):
    return jax.shard_map(
        per_device,
        mesh=mesh,
        in_specs=(
            P(None, "patch", None),
            P(None, "patch", "chan"),
            P(None, "patch", "chan"),
            P(None, "chan"),
            P(None, "chan"),
            P(None, "chan"),
            P("chan", None),
            P(None, "chan"),
            P(None, "chan"),
            P("chan", None),
        ),
        out_specs=P(None, "patch", "chan"),
        check_vma=False,
    )
```

profile of v0, /device:TPU:1, one launch (start us, length us, event | category | flops | bytes accessed | tf_op | source)
XLA Modules:
  0.0 263.5 jit_solution(2626598971788410066)
XLA Ops:
  6.5 1.2 copy.27
  7.7 1.0 copy.28
  15.3 83.2 %all-gather.2.cloned.1.call-done = bf16[2,16384,128]{1,2,0:T(8,128)(2,1)} async-done(((bf16[2,512,128]{1,2,0:T(8,128)(2,1)}), bf16[2,16384,128]{1,2,0:T(8,128)(2,1)}) %all-gather.2.cloned.1.call-update) | async-done | bytes 8388624 | tf_op jit(solution)/shard_map/all_gather | solution.py:11
  98.5 5.8 %fusion.112 = (bf16[1,16384,128]{1,2,0:T(8,128)(2,1)}, bf16[1,16384,128]{1,2,0:T(8,128)(2,1)}) fusion(bf16[2,16384,128]{1,2,0:T(8,128)(2,1)} %all-gather.2.cloned.1.call-done), kind=kLoop, calls=%fused_computation.157 | loop fusion | bytes 16777216 | tf_op jit(solution)/shard_map/slice | solution.py:13
  104.3 68.7 %while.19 = (s32[]{:T(128)}, f32[1,2,512,64]{2,3,1,0:T(8,128)S(1)}, f32[1,2,512]{2,1,0:T(2,128)S(1)}, f32[1,2,512]{2,1,0:T(2,128)S(1)}, s32[]{:T(128)}, /*index=...) while((s32[]{:T(128)}, f32[1,2,512,64]{2,3,1,0:T(8,128)S(1)}, ...), condition=%wide.region_7.8_spmd, body=%wide.region_4.7_spmd.sunk | while | flops 280121344 | bytes 14880943 | solution.py:111
  104.3 1.1 constant_dynamic-slice_fusion.4
  105.4 1.1 bitcast_reduce_fusion.2
  106.5 1.1 fusion.144
  108.6 1.1 constant_dynamic-slice_fusion.4
  109.7 1.1 bitcast_reduce_fusion.2
  110.8 1.1 fusion.144
  112.9 1.1 constant_dynamic-slice_fusion.4
  114.0 1.1 bitcast_reduce_fusion.2
  115.1 1.1 fusion.144
  117.2 1.1 constant_dynamic-slice_fusion.4
  118.3 1.1 bitcast_reduce_fusion.2
  119.4 1.1 fusion.144
  121.5 1.1 constant_dynamic-slice_fusion.4
  122.6 1.1 bitcast_reduce_fusion.2
  123.6 1.1 fusion.144
  125.8 1.1 constant_dynamic-slice_fusion.4
  126.9 1.1 bitcast_reduce_fusion.2
  127.9 1.1 fusion.144
  130.1 1.1 constant_dynamic-slice_fusion.4
  131.2 1.1 bitcast_reduce_fusion.2
  132.2 1.1 fusion.144
  134.4 1.1 constant_dynamic-slice_fusion.4
  135.5 1.1 bitcast_reduce_fusion.2
  136.5 1.1 fusion.144
  138.7 1.1 constant_dynamic-slice_fusion.4
  139.7 1.1 bitcast_reduce_fusion.2
  140.8 1.1 fusion.144
  143.0 1.1 constant_dynamic-slice_fusion.4
  144.0 1.1 bitcast_reduce_fusion.2
  145.1 1.1 fusion.144
  147.3 1.1 constant_dynamic-slice_fusion.4
  148.3 1.1 bitcast_reduce_fusion.2
  149.4 1.1 fusion.144
  151.6 1.1 constant_dynamic-slice_fusion.4
  152.6 1.1 bitcast_reduce_fusion.2
  153.7 1.1 fusion.144
  155.9 1.1 constant_dynamic-slice_fusion.4
  156.9 1.1 bitcast_reduce_fusion.2
  158.0 1.1 fusion.144
  160.1 1.1 constant_dynamic-slice_fusion.4
  161.2 1.1 bitcast_reduce_fusion.2
  162.3 1.1 fusion.144
  164.4 1.1 constant_dynamic-slice_fusion.4
  165.5 1.1 bitcast_reduce_fusion.2
  166.6 1.1 fusion.144
  168.7 1.1 constant_dynamic-slice_fusion.4
  169.8 1.1 bitcast_reduce_fusion.2
  170.9 1.1 fusion.144
  173.0 2.6 convolution_convert_fusion.1
  175.6 2.4 copy.29
  178.1 4.3 %all-to-all-start = ((bf16[8,1,512,160]{2,3,1,0:T(8,128)(2,1)}), bf16[8,1,512,160]{2,3,1,0:T(8,128)(2,1)}, u32[]{:S(2)}, u32[]{:S(2)}) async-start(bf16[8,1,512,160]{2,3,1,0:T(8,128)(2,1)} %bitcast.139), calls=%async_computation | async-start | bytes 2621440 | tf_op jit(solution)/shard_map/all_to_all | solution.py:25
  182.6 17.5 %all-to-all-done = bf16[8,1,512,160]{2,3,1,0:T(8,128)(2,1)} async-done(((bf16[8,1,512,160]{2,3,1,0:T(8,128)(2,1)}), bf16[8,1,512,160]{2,3,1,0:T(8,128)(2,1)}, u32[]{:S(2)}, u32[]{:S(2)}) %all-to-all-start) | async-done | bytes 1310752 | tf_op jit(solution)/shard_map/all_to_all | solution.py:25
  200.1 1.5 convert_reduce_fusion.2
  201.8 20.6 %all_to_all.15 = bf16[8,1,512,160]{2,3,1,0:T(8,128)(2,1)S(1)} all-to-all(bf16[8,1,512,160]{2,3,1,0:T(8,128)(2,1)S(1)} %broadcast_in_dim.54), channel_id=1, replica_groups=mesh['patch'=32,'chan'=8] {'chan'}, dimensions={0} | all-to-all | bytes 2621440 | tf_op jit(solution)/shard_map/all_to_all | solution.py:37
  223.8 1.0 copy-done.5
  224.8 2.3 fusion.113
  227.1 7.6 %convolution_convert_fusion = bf16[512,1280]{1,0:T(8,128)(2,1)} fusion(bf16[640,1280]{1,0:T(8,128)(2,1)S(1)} %copy-done, bf16[512,1280]{0,1:T(8,128)(2,1)S(1)} %fusion.28, bf16[1280,640]{1,0:T(8,128)(2,1)} %param.19, f32[512,640]{1,0:T(8,128)} %fusion.113), kind=kOutput, calls=%fused_computation.34 | convolution fusion | flops 1700003840 | bytes 7208960 | tf_op jit(solution)/shard_map/btd,de->bte/dot_general | solution.py:52
  234.7 1.6 copy.32
  236.3 19.4 %all_to_all.16 = bf16[8,1,512,160]{2,3,1,0:T(8,128)(2,1)S(1)} all-to-all(bf16[8,1,512,160]{2,3,1,0:T(8,128)(2,1)S(1)} %bitcast.140), channel_id=1, replica_groups=mesh['patch'=32,'chan'=8] {'chan'}, dimensions={0} | all-to-all | bytes 2621440 | tf_op jit(solution)/shard_map/all_to_all | solution.py:25
  (120 shorter events, 24.6 us)
Async XLA Ops:
  6.5 220.6 %copy-start = (bf16[640,1280]{1,0:T(8,128)(2,1)S(1)}, bf16[640,1280]{1,0:T(8,128)(2,1)}, u32[]{:S(2)}) copy-start(bf16[640,1280]{1,0:T(8,128)(2,1)} %param.21) | copy-start | bytes 4915204
  6.5 2.9 %copy-start.1 = (bf16[1,512,1280]{2,1,0:T(8,128)(2,1)S(1)}, bf16[1,512,1280]{2,1,0:T(8,128)(2,1)}, u32[]{:S(2)}) copy-start(bf16[1,512,1280]{2,1,0:T(8,128)(2,1)} %param.12) | copy-start | bytes 3932164
  6.5 92.0 %all-gather.2.cloned.1.call-start = ((), (), s32[]{:S(2)}) async-start(), calls=%async_computation.3 | async-start | bytes 8650752 | tf_op jit(solution)/shard_map/all_gather | solution.py:11
  10.2 1.0 copy-start.2
  11.2 1.0 copy-start.3
  13.3 1.0 copy-start.4
  178.1 22.0 %all-to-all-start = ((bf16[8,1,512,160]{2,3,1,0:T(8,128)(2,1)}), bf16[8,1,512,160]{2,3,1,0:T(8,128)(2,1)}, u32[]{:S(2)}, u32[]{:S(2)}) async-start(bf16[8,1,512,160]{2,3,1,0:T(8,128)(2,1)} %bitcast.139), calls=%async_computation | async-start | bytes 2621440 | tf_op jit(solution)/shard_map/all_to_all | solution.py:25
  223.4 1.4 copy-start.5
Sparse Core Ops, SparseCore 0:
  9.8 88.6 all-gather.1
where the time goes:
time: 266 us; the launch traced here: 264 us
  waiting for transfers between devices  101 us (38%)
  matrix products  50.3 us (19%)
  blocking collectives  40 us (15%)
  local copies, waits for them, and re-layouts  32.2 us (12%)
  other arithmetic  21.4 us (8%)
  between operations  13.6 us (5%)
  starting transfers between devices  4.27 us (2%)
    all_gather x1, waiting for transfers between devices, in_one_piece(): result, at, done = (lax.all_gather(both, axis, axis=dim, tiled=True), 0, [])  83.2 us
    all_to_all x1, blocking collectives, from_everyone(): return lax.all_to_all(copies, axis, split_axis=0, concat_axis=0, tiled=True)  20.6 us
    all_to_all x1, blocking collectives, sent_and_summed(): lax.all_to_all(split_up(shard, dim, devices), axis, 0, 0, tiled=True)  19.4 us
    dot_general x17, matrix products, attend(): jnp.einsum('bhqk,bkhd->bhqd', weights.astype(jnp.bfloat16), value_rows, p...  18.8 us
    all_to_all x1, waiting for transfers between devices, sent_and_summed(): lax.all_to_all(split_up(shard, dim, devices), axis, 0, 0, tiled=True)  17.5 us
    dot_general x17, matrix products, attend(): jnp.einsum('bqhd,bkhd->bhqk', queries, key_rows, preferred_element_type=j...  17.3 us
    dynamic_slice x16, local copies, waits for them, and re-layouts, turn(): value_block = lax.dynamic_slice_in_dim(value_rows, offset, 1024, 1)  17.2 us
    reduce_sum x17, other arithmetic, attend(): totals = totals * rescale + jnp.sum(weights, axis=-1)  15 us
  transfers between devices with their start and end apart: 2, of which 2 were waited for; matrix products, arithmetic and copies ran while one was open for 2% of the time, Pallas kernels for 0%

commit v1 on v0

v1 whole, which is shorter than its diff:
```python
import functools
import math

import jax
import jax.numpy as jnp
from jax import lax
from jax.experimental import pallas as pl
from jax.experimental.pallas import tpu as pltpu
from jax.sharding import PartitionSpec as P

HD = 64
MESH = pl.DeviceIdType.MESH
F32 = jnp.float32
BF16 = jnp.bfloat16
LOW = -1e30
SCALE = math.log2(math.e) / math.sqrt(HD)


def normalize(values):
    mean = jnp.mean(values, axis=-1, keepdims=True)
    centered = values - mean
    var = jnp.mean(centered * centered, axis=-1, keepdims=True)
    return centered * lax.rsqrt(var + 1e-05)


def attention_kernel(
    tok, k_in, v_in, w_q, w_k, w_v, out,
    normed, kvb, kvo, qb, qo, kk, qq, s_a, s_b, b_a, b_b,
    top, total, acc, stat_out, o_out, o_in, stat_in, fin,
    kv_send, kv_recv, q_send, q_recv, o_send, o_recv, t_send, t_recv,
):
    p, c = lax.axis_index("patch"), lax.axis_index("chan")
    s = lax.rem(p, 2)
    z = lax.rem(lax.div(p, 2), 4)
    y = lax.div(p, 8)
    t = 1 - s
    y_up, y_down = lax.rem(y + 1, 4), lax.rem(y + 3, 4)
    z_up, z_down = lax.rem(z + 1, 4), lax.rem(z + 3, 4)

    def dev(y, z, s):
        return ((y * 4 + z) * 2 + s, c)

    partner = dev(y, z, t)
    rows = tok.shape[0]

    barrier = pltpu.get_barrier_semaphore()
    peers = [partner]
    for core in (s, t):
        peers += [dev(y_up, z, core), dev(y_down, z, core)]
        peers += [dev(y, z_up, core), dev(y, z_down, core)]
    for peer in peers:
        pl.semaphore_signal(barrier, inc=1, device_id=peer, device_id_type=MESH)
    pl.semaphore_wait(barrier, len(peers))

    def split_heads(values):
        first, second = values[:HD], values[HD:]
        mine = jnp.where(s == 0, first, second)
        other = jnp.where(s == 0, second, first)
        return mine, other

    def copy(src, dst, send, recv, peer):
        return pltpu.make_async_remote_copy(
            src_ref=src, dst_ref=dst, send_sem=send, recv_sem=recv,
            device_id=peer, device_id_type=MESH,
        )

    for j, ref in enumerate((k_in, v_in)):
        mine, other = split_heads(ref[...].T)
        kvb[0, j] = mine
        kvo[0, j] = other
    kv = {
        2: copy(kvb.at[0], kvb.at[2], kv_send.at[2], kv_recv.at[2], dev(y_up, z, s)),
        3: copy(kvo.at[0], kvb.at[3], kv_send.at[3], kv_recv.at[3], dev(y_down, z, t)),
        1: copy(kvo.at[0], kvb.at[1], kv_send.at[1], kv_recv.at[1], partner),
        4: copy(kvo.at[0], kvb.at[4], kv_send.at[4], kv_recv.at[4], dev(y_up, z, t)),
        5: copy(kvb.at[0], kvb.at[5], kv_send.at[5], kv_recv.at[5], dev(y_down, z, s)),
        6: copy(kvb.at[2], kvb.at[6], kv_send.at[6], kv_recv.at[6], dev(y_up, z, s)),
        7: copy(kvb.at[3], kvb.at[7], kv_send.at[7], kv_recv.at[7], dev(y_down, z, s)),
        9: copy(kvo.at[1], kvb.at[9], kv_send.at[9], kv_recv.at[9], partner),
    }
    for j in (2, 3, 1, 4, 5):
        kv[j].start()

    step = 128

    def norm_rows(i, _):
        at = pl.ds(pl.multiple_of(i * step, step), step)
        normed[at, :] = normalize(tok[at, :].astype(F32)).astype(BF16)
        return 0

    lax.fori_loop(0, rows // step, norm_rows, 0)

    def project(w):
        return jnp.dot(normed[...], w[...], preferred_element_type=F32).astype(BF16)

    mine, other = split_heads(project(w_q).T)
    qb[0] = mine
    qo[...] = other
    q = {
        2: copy(qb.at[0], qb.at[2], q_send.at[2], q_recv.at[2], dev(y, z_up, s)),
        3: copy(qo, qb.at[3], q_send.at[3], q_recv.at[3], dev(y, z_down, t)),
        4: copy(qo, qb.at[4], q_send.at[4], q_recv.at[4], dev(y, z_up, t)),
        5: copy(qb.at[0], qb.at[5], q_send.at[5], q_recv.at[5], dev(y, z_down, s)),
        1: copy(qo, qb.at[1], q_send.at[1], q_recv.at[1], partner),
        6: copy(qb.at[2], qb.at[6], q_send.at[6], q_recv.at[6], dev(y, z_up, s)),
        7: copy(qb.at[3], qb.at[7], q_send.at[7], q_recv.at[7], dev(y, z_down, s)),
    }
    for j in (2, 3, 4, 5, 1):
        q[j].start()
    for j, w in enumerate((w_k, w_v)):
        mine, other = split_heads(project(w).T)
        kvb[8, j] = mine
        kvo[1, j] = other
    kv[9].start()

    top[...] = jnp.full(top.shape, LOW, F32)
    total[...] = jnp.zeros(total.shape, F32)
    acc[...] = jnp.zeros(acc.shape, F32)

    def prepare_keys(u):
        key = kvb[u, 0]
        kk[u] = jnp.concatenate([key, key], axis=0).T

    def prepare_queries(f):
        scaled = qb[f].astype(F32) * SCALE
        high = scaled.astype(BF16)
        low = (scaled - high.astype(F32)).astype(BF16)
        qq[f] = jnp.concatenate([high, low], axis=0)

    def score(f, u, s_ref, b_ref):
        values = jnp.dot(kk[u], qq[f], preferred_element_type=F32)
        s_ref[...] = values
        b_ref[...] = jnp.max(values, axis=0, keepdims=True)

    def absorb(f, u, s_ref, b_ref):
        old = top[f]
        new = jnp.maximum(old, b_ref[...])
        rescale = jnp.exp2(old - new)
        weights = jnp.exp2(s_ref[...] - new)
        total[f] = total[f] * rescale + jnp.sum(weights, axis=0, keepdims=True)
        acc[f] = acc[f] * rescale + jnp.dot(
            kvb[u, 1], weights.astype(BF16), preferred_element_type=F32
        )
        top[f] = new

    def attend(count, pair):
        score(*pair(0), s_a, b_a)

        def two(i, _):
            first, second = pair(2 * i), pair(2 * i + 1)
            third = pair(jnp.minimum(2 * i + 2, count - 1))
            score(*second, s_b, b_b)
            absorb(*first, s_a, b_a)
            score(*third, s_a, b_a)
            absorb(*second, s_b, b_b)
            return 0

        lax.fori_loop(0, count // 2, two, 0)

    def block(f0, nf, u0, nu):
        attend(nf * nu, lambda i: (f0 + lax.div(i, nu), u0 + lax.rem(i, nu)))

    def own_pair(i):
        f, b = lax.div(i, 2), lax.rem(i, 2)
        return f, b + 8 * (1 - f - b + 2 * f * b)

    prepare_keys(0)
    prepare_keys(8)
    prepare_queries(0)
    kv[1].wait_recv()
    prepare_keys(1)
    q[1].wait_recv()
    prepare_queries(1)
    kv[9].wait_recv()
    prepare_keys(9)
    attend(4, lambda i: own_pair(jnp.int32(i)))

    for j in (2, 3):
        kv[j].wait_recv()
        kv[j + 4].start()
        prepare_keys(j)
    block(0, 2, 2, 2)

    for j in (2, 3):
        q[j].wait_recv()
        q[j + 4].start()
        prepare_queries(j)
    for j in (4, 5):
        kv[j].wait_recv()
        prepare_keys(j)
    block(2, 2, 0, 6)

    for j in (4, 5):
        q[j].wait_recv()
        prepare_queries(j)
    block(4, 2, 0, 6)

    for j in (6, 7):
        kv[j].wait_recv()
        prepare_keys(j)
        q[j].wait_recv()
        prepare_queries(j)
    block(6, 2, 0, 8)

    targets = {
        6: (dev(y, z_up, s), 5),
        7: (dev(y, z_down, s), 6),
        2: (dev(y, z_down, s), 1),
        3: (dev(y, z_up, t), 2),
        4: (dev(y, z_down, t), 3),
        5: (dev(y, z_up, s), 4),
        1: (partner, 0),
    }
    back = {}
    for f, (peer, slot) in targets.items():
        back[f] = (
            copy(o_out.at[f], o_in.at[slot], o_send.at[f], o_recv.at[slot], peer),
            copy(stat_out.at[f], stat_in.at[slot], t_send.at[f], t_recv.at[slot], peer),
        )

    def give(f):
        o_out[f] = acc[f].astype(BF16)
        stat_out[f, 0:1] = top[f]
        stat_out[f, 1:2] = total[f]
        for part in back[f]:
            part.start()

    def arrived(f):
        for part in back[f]:
            part.wait_recv()

    def merge(one, other):
        new = jnp.maximum(one[0], other[0])
        left, right = jnp.exp2(one[0] - new), jnp.exp2(other[0] - new)
        return (
            new,
            one[1] * left + other[1] * right,
            one[2] * left + other[2] * right,
        )

    def received(slot):
        return (
            stat_in[slot, 0:1], stat_in[slot, 1:2], o_in[slot].astype(F32),
        )

    def local(f):
        return top[f], total[f], acc[f]

    give(6)
    give(7)
    block(2, 4, 6, 2)
    give(2)
    give(3)
    arrived(6)
    arrived(7)
    for f, slot in ((5, 5), (4, 6)):
        top[f], total[f], acc[f] = merge(local(f), received(slot))
        give(f)
    block(1, 1, 4, 4)
    give(1)
    block(0, 1, 4, 4)

    for f in (1, 2, 3, 4, 5):
        arrived(f)
    _, sums, values = merge(merge(local(0), received(1)), received(4))
    fin[s] = values / sums
    _, sums, values = merge(merge(received(0), received(2)), received(3))
    fin[t] = values / sums
    out[...] = jnp.concatenate([fin[0], fin[1]], axis=0).T.astype(BF16)

    for j in (1, 2, 3, 4, 5, 6, 7, 9):
        kv[j].wait_send()
    for j in (1, 2, 3, 4, 5, 6, 7):
        q[j].wait_send()
        for part in back[j]:
            part.wait_send()


def attention(tokens, stale_k, stale_v, w_query, w_key, w_value):
    rows, width = tokens.shape
    vmem = pl.BlockSpec(memory_space=pltpu.VMEM)
    dma = pltpu.SemaphoreType.DMA
    return pl.pallas_call(
        attention_kernel,
        out_shape=jax.ShapeDtypeStruct((rows, 2 * HD), BF16),
        in_specs=[vmem] * 6,
        out_specs=vmem,
        scratch_shapes=[
            pltpu.VMEM((rows, width), BF16),
            pltpu.VMEM((10, 2, HD, rows), BF16),
            pltpu.VMEM((2, 2, HD, rows), BF16),
            pltpu.VMEM((8, HD, rows), BF16),
            pltpu.VMEM((HD, rows), BF16),
            pltpu.VMEM((10, rows, 2 * HD), BF16),
            pltpu.VMEM((8, 2 * HD, rows), BF16),
            pltpu.VMEM((rows, rows), F32),
            pltpu.VMEM((rows, rows), F32),
            pltpu.VMEM((1, rows), F32),
            pltpu.VMEM((1, rows), F32),
            pltpu.VMEM((8, 1, rows), F32),
            pltpu.VMEM((8, 1, rows), F32),
            pltpu.VMEM((8, HD, rows), F32),
            pltpu.VMEM((8, 2, rows), F32),
            pltpu.VMEM((8, HD, rows), BF16),
            pltpu.VMEM((7, HD, rows), BF16),
            pltpu.VMEM((7, 2, rows), F32),
            pltpu.VMEM((2, HD, rows), F32),
            dma((10,)), dma((10,)), dma((8,)), dma((8,)),
            dma((8,)), dma((7,)), dma((8,)), dma((7,)),
        ],
        compiler_params=pltpu.CompilerParams(collective_id=0, has_side_effects=True),
    )(tokens, stale_k, stale_v, w_query, w_key, w_value)


def split_up(shard, dim, devices):
    before, after = (shard.shape[:dim], shard.shape[dim + 1 :])
    return jnp.moveaxis(shard.reshape(*before, devices, -1, *after), dim, 0)


def sent_and_summed(shard, axis, dim):
    devices = lax.axis_size(axis)
    pieces = lax.all_to_all(split_up(shard, dim, devices), axis, 0, 0, tiled=True)
    return jnp.sum(pieces.astype(jnp.float32), axis=0)


def in_order(pieces, dim):
    lengths = list(pieces.shape[1:])
    lengths[dim] *= pieces.shape[0]
    return jnp.moveaxis(pieces, 0, dim).reshape(lengths)


def from_everyone(shard, axis):
    copies = jnp.broadcast_to(shard, (lax.axis_size(axis), *shard.shape))
    return lax.all_to_all(copies, axis, split_axis=0, concat_axis=0, tiled=True)


def collect(shard, axis, dim):
    return in_order(from_everyone(shard, axis), dim)


def project(inputs, weight):
    return jnp.einsum("btd,de->bte", inputs, weight, preferred_element_type=jnp.float32)


def per_device(
    tokens, stale_k, stale_v, w_query, w_key, w_value, w_out, ff_value, ff_gate, ff_down
):
    batch_size, row_count, width = tokens.shape
    attended = attention(
        tokens[0], stale_k[0], stale_v[0], w_query, w_key, w_value
    )[None]
    partial_value = project(attended, w_out)
    chan_id = lax.axis_index("chan")
    share_width = width // lax.axis_size("chan")
    attn_part = sent_and_summed(partial_value.astype(jnp.bfloat16), "chan", 2)
    resid_share = (
        lax.dynamic_slice_in_dim(tokens, chan_id * share_width, share_width, 2).astype(jnp.float32)
        + attn_part
    )
    resid = collect(resid_share.astype(jnp.bfloat16), "chan", 2).astype(resid_share.dtype)
    normed_two = normalize(resid).astype(jnp.bfloat16)
    ff_val = project(normed_two, ff_value)
    gate_out = project(normed_two, ff_gate)
    gated = (ff_val * jax.nn.gelu(gate_out, approximate=False)).astype(jnp.bfloat16)
    down_out = project(gated, ff_down)
    ffn_part = sent_and_summed(down_out.astype(jnp.bfloat16), "chan", 2)
    return (resid_share + ffn_part).astype(jnp.bfloat16)


def solution(mesh):
    return jax.shard_map(
        per_device,
        mesh=mesh,
        in_specs=(
            P(None, "patch", None),
            P(None, "patch", "chan"),
            P(None, "patch", "chan"),
            P(None, "chan"),
            P(None, "chan"),
            P(None, "chan"),
            P("chan", None),
            P(None, "chan"),
            P(None, "chan"),
            P("chan", None),
        ),
        out_specs=P(None, "patch", "chan"),
        check_vma=False,
    )
```

time: 266 us -> 128 us (0.48)
  waiting for transfers between devices: 101 us -> 16.5 us
  Pallas kernels: 0 us -> 46.2 us
  matrix products: 50.3 us -> 11.3 us
  local copies, waits for them, and re-layouts: 32.2 us -> 5.51 us
  other arithmetic: 21.4 us -> 2.46 us
  between operations: 13.6 us -> 0.1 us
    all_gather x1 -> x0, waiting for transfers between devices: 83.2 us -> none  [in_one_piece(): result, at, done = (lax.all_gather(both, axis, axis=dim, tiled=True), 0, [])]
    pallas_call x0 -> x1, Pallas kernels: none -> 46.2 us  [attention(): pl.pallas_call(attention_kernel, out_shape=jax.ShapeDtypeStruct((rows, 2...]
    dot_general x34 -> x0, matrix products: 36.1 us -> none  [the longest x17 18.8 us: attend(): jnp.einsum('bhqk,bkhd->bhqd', weights.astype(jnp.bfloat16), value_rows, p...]
    dynamic_slice x16 -> x0, local copies, waits for them, and re-layouts: 17.2 us -> none  [turn(): value_block = lax.dynamic_slice_in_dim(value_rows, offset, 1024, 1)]
    reduce_sum x21 -> x2, other arithmetic: 16.3 us -> 0.59 us  [the longest x1 0.34 us: normalize(): var = jnp.mean(centered * centered, axis=-1, keepdims=True)]
    slice x1 -> x0, local copies, waits for them, and re-layouts: 5.81 us -> none  [in_one_piece(): done.append(lax.slice_in_dim(result, at, at + a.shape[along], axis=along))]
    unnamed x15 -> x7, local copies, waits for them, and re-layouts: 4.92 us -> 1.17 us
    dot_general x6 -> x3, matrix products: 14.2 us -> 11.3 us  [project(): jnp.einsum('btd,de->bte', inputs, weight, preferred_element_type=jnp.floa...]
  transfers between devices with their start and end apart: 2 -> 1, of which waited for: 2 -> 1; matrix products, arithmetic and copies ran while one was open for 2% -> 1% of each run, Pallas kernels for 0% -> 0%
where the time goes in v1:
time: 128 us; the launch traced here: 126 us
  Pallas kernels  46.2 us (36%)
  blocking collectives  39.3 us (31%)
  waiting for transfers between devices  16.5 us (13%)
  matrix products  11.3 us (9%)
  local copies, waits for them, and re-layouts  5.51 us (4%)
  starting transfers between devices  4.69 us (4%)
  other arithmetic  2.46 us (2%)
    pallas_call x1, Pallas kernels, attention(): pl.pallas_call(attention_kernel, out_shape=jax.ShapeDtypeStruct((rows, 2...  46.2 us
    all_to_all x1, blocking collectives, from_everyone(): return lax.all_to_all(copies, axis, split_axis=0, concat_axis=0, tiled=True)  20.6 us
    all_to_all x1, blocking collectives, sent_and_summed(): lax.all_to_all(split_up(shard, dim, devices), axis, 0, 0, tiled=True)  18.6 us
    all_to_all x1, waiting for transfers between devices, sent_and_summed(): lax.all_to_all(split_up(shard, dim, devices), axis, 0, 0, tiled=True)  16.5 us
    dot_general x3, matrix products, project(): jnp.einsum('btd,de->bte', inputs, weight, preferred_element_type=jnp.floa...  11.3 us
    all_to_all x1, starting transfers between devices, sent_and_summed(): lax.all_to_all(split_up(shard, dim, devices), axis, 0, 0, tiled=True)  4.69 us
  transfers between devices with their start and end apart: 1, of which 1 were waited for; matrix products, arithmetic and copies ran while one was open for 1% of the time, Pallas kernels for 0%

profile of v1, /device:TPU:1, one launch (start us, length us, event | category | flops | bytes accessed | tf_op | source)
XLA Modules:
  0.0 126.0 jit_solution(10199562762060379476)
XLA Ops:
  0.0 0.0 copy-start
  0.0 0.0 copy-start.1
  0.0 46.2 %shard_map.100 = bf16[512,128]{1,0:T(8,128)(2,1)} custom-call(bf16[512,1280]{1,0:T(8,128)(2,1)} %bitcast.55, bf16[512,128]{1,0:T(8,128)(2,1)} %bitcast.56, bf16[512,128]{1,0:T(8,128)(2,1)} %bitcast.57, bf16[1280,128]{1,0:T(8,128)(2,1)} %w_q.1, bf16[1280,128]{1,0:T(8,128)(2,1)} %w_k.1, bf16[1280,128]{1,0:T(8,128)(2,1)} %w_v.1), custom_call_target="tpu_custom_call" | custom-call | tf_op jit(solution)/shard_map/pallas_call | solution.py:283
  46.2 0.0 copy-done.1
  46.2 1.4 %convolution_convert_fusion.1 = bf16[512,1280]{1,0:T(8,128)(2,1)S(1)} fusion(bf16[512,128]{1,0:T(8,128)(2,1)} %shard_map.100, bf16[128,1280]{1,0:T(8,128)(2,1)S(1)} %copy-done.1), kind=kOutput, calls=%fused_computation.1 | convolution fusion | flops 168427520 | bytes 1769472 | tf_op jit(solution)/shard_map/btd,de->bte/dot_general | solution.py:342
  47.6 1.5 %copy.17 = bf16[512,1280]{0,1:T(8,128)(2,1)} copy(bf16[512,1280]{1,0:T(8,128)(2,1)S(1)} %convolution_convert_fusion.1) | data formatting | bytes 2621440 | tf_op jit(solution)/shard_map/convert_element_type | solution.py:355
  49.1 4.7 %all-to-all-start = ((bf16[8,1,512,160]{2,3,1,0:T(8,128)(2,1)}), bf16[8,1,512,160]{2,3,1,0:T(8,128)(2,1)S(1)}, u32[]{:S(2)}, u32[]{:S(2)}) async-start(bf16[8,1,512,160]{2,3,1,0:T(8,128)(2,1)} %bitcast.53), calls=%async_computation | async-start | bytes 2621440 | tf_op jit(solution)/shard_map/all_to_all | solution.py:322
  53.8 1.1 constant_dynamic-slice_fusion
  55.0 0.1 copy.22
  55.1 16.5 %all-to-all-done = bf16[8,1,512,160]{2,3,1,0:T(8,128)(2,1)S(1)} async-done(((bf16[8,1,512,160]{2,3,1,0:T(8,128)(2,1)}), bf16[8,1,512,160]{2,3,1,0:T(8,128)(2,1)S(1)}, u32[]{:S(2)}, u32[]{:S(2)}) %all-to-all-start) | async-done | bytes 1310752 | tf_op jit(solution)/shard_map/all_to_all | solution.py:322
  71.6 0.2 convert_reduce_fusion.1
  71.8 0.1 broadcast_in_dim.2
  71.9 20.6 %all_to_all.15 = bf16[8,1,512,160]{2,3,1,0:T(8,128)(2,1)S(1)} all-to-all(bf16[8,1,512,160]{2,3,1,0:T(8,128)(2,1)S(1)} %broadcast_in_dim.2), channel_id=1, replica_groups=mesh['patch'=32,'chan'=8] {'chan'}, dimensions={0} | all-to-all | bytes 2621440 | tf_op jit(solution)/shard_map/all_to_all | solution.py:334
  92.6 0.2 fusion.14
  92.8 0.3 bitcast_convert_fusion
  93.2 0.3 fusion.1
  93.5 0.0 copy-start.2
  93.5 0.4 fusion.3
  93.9 1.0 copy-done.2
  95.0 2.3 %fusion.78 = f32[512,640]{1,0:T(8,128)} fusion(bf16[512,1280]{0,1:T(8,128)(2,1)S(1)} %fusion.3, bf16[1280,640]{1,0:T(8,128)(2,1)S(1)} %copy-done.2), kind=kOutput, calls=%fused_computation.100 | convolution fusion | flops 838860800 | bytes 4259840 | tf_op jit(solution)/shard_map/btd,de->bte/dot_general | solution.py:342
  97.2 0.0 copy-done
  97.3 7.6 %convolution_convert_fusion = bf16[512,1280]{1,0:T(8,128)(2,1)} fusion(bf16[640,1280]{1,0:T(8,128)(2,1)S(1)} %copy-done, bf16[512,1280]{0,1:T(8,128)(2,1)S(1)} %fusion.3, bf16[1280,640]{1,0:T(8,128)(2,1)} %param.17, f32[512,640]{1,0:T(8,128)} %fusion.78), kind=kOutput, calls=%fused_computation | convolution fusion | flops 1700003840 | bytes 7208960 | tf_op jit(solution)/shard_map/btd,de->bte/dot_general | solution.py:342
  104.9 1.6 %copy.20 = bf16[512,1280]{0,1:T(8,128)(2,1)S(1)} copy(bf16[512,1280]{1,0:T(8,128)(2,1)} %convolution_convert_fusion) | data formatting | bytes 2621440 | tf_op jit(solution)/shard_map/convert_element_type | solution.py:366
  106.5 18.6 %all_to_all.16 = bf16[8,1,512,160]{2,3,1,0:T(8,128)(2,1)S(1)} all-to-all(bf16[8,1,512,160]{2,3,1,0:T(8,128)(2,1)S(1)} %bitcast.54), channel_id=1, replica_groups=mesh['patch'=32,'chan'=8] {'chan'}, dimensions={0} | all-to-all | bytes 2621440 | tf_op jit(solution)/shard_map/all_to_all | solution.py:322
  125.1 0.2 convert_reduce_fusion
  125.3 0.7 fusion.45
  (3 shorter events, 0.1 us)
Async XLA Ops:
  0.0 97.2 %copy-start = (bf16[640,1280]{1,0:T(8,128)(2,1)S(1)}, bf16[640,1280]{1,0:T(8,128)(2,1)}, u32[]{:S(2)}) copy-start(bf16[640,1280]{1,0:T(8,128)(2,1)} %param.19) | copy-start | bytes 4915204
  0.0 46.2 %copy-start.1 = (bf16[128,1280]{1,0:T(8,128)(2,1)S(1)}, bf16[128,1280]{1,0:T(8,128)(2,1)}, u32[]{:S(2)}) copy-start(bf16[128,1280]{1,0:T(8,128)(2,1)} %param.16) | copy-start | bytes 983044
  49.1 22.5 %all-to-all-start = ((bf16[8,1,512,160]{2,3,1,0:T(8,128)(2,1)}), bf16[8,1,512,160]{2,3,1,0:T(8,128)(2,1)S(1)}, u32[]{:S(2)}, u32[]{:S(2)}) async-start(bf16[8,1,512,160]{2,3,1,0:T(8,128)(2,1)} %bitcast.53), calls=%async_computation | async-start | bytes 2621440 | tf_op jit(solution)/shard_map/all_to_all | solution.py:322
  93.5 1.4 %copy-start.2 = (bf16[1280,640]{1,0:T(8,128)(2,1)S(1)}, bf16[1280,640]{1,0:T(8,128)(2,1)}, u32[]{:S(2)}) copy-start(bf16[1280,640]{1,0:T(8,128)(2,1)} %param.18) | copy-start | bytes 4915204

commit v2 on v1

v2 whole, which is shorter than its diff:
```python
import functools
import math

import jax
import jax.numpy as jnp
from jax import lax
from jax.experimental import pallas as pl
from jax.experimental.pallas import tpu as pltpu
from jax.sharding import PartitionSpec as P

HD = 64
MESH = pl.DeviceIdType.MESH
F32 = jnp.float32
BF16 = jnp.bfloat16
LOW = -1e30
SCALE = math.log2(math.e) / math.sqrt(HD)


def normalize(values):
    mean = jnp.mean(values, axis=-1, keepdims=True)
    centered = values - mean
    var = jnp.mean(centered * centered, axis=-1, keepdims=True)
    return centered * lax.rsqrt(var + 1e-05)


def block_kernel(
    tok_hbm, k_hbm, v_hbm, wq_hbm, wk_hbm, wv_hbm, wo_hbm, fv_hbm, fg_hbm, fd_hbm, out,
    tok, k_in, v_in, w_q, w_k, w_v, w_o, f_v, f_g, f_d,
    normed, kvb, kvo, qb, qo, kk, qq, s_a, s_b, b_a, b_b,
    top, total, acc, stat_out, o_out, o_in, stat_in, fin,
    att, resid, turned, down, pieces,
    load, kv_send, kv_recv, q_send, q_recv, o_send, o_recv, t_send, t_recv,
    w_send, w_recv, wx_send, wx_recv, a_send, a_recv, r_send, r_recv,
):
    p, c = lax.axis_index("patch"), lax.axis_index("chan")
    s = lax.rem(p, 2)
    z = lax.rem(lax.div(p, 2), 4)
    y = lax.div(p, 8)
    t = 1 - s
    y_up, y_down = lax.rem(y + 1, 4), lax.rem(y + 3, 4)
    z_up, z_down = lax.rem(z + 1, 4), lax.rem(z + 3, 4)
    across, along = lax.div(c, 4), lax.rem(c, 4)
    rows = tok.shape[0]
    half = rows // 2
    share = out.shape[1]

    def dev(y, z, s):
        return ((y * 4 + z) * 2 + s, c)

    partner = dev(y, z, t)

    def chan_of(j):
        return lax.rem(across + j // 4, 2) * 4 + lax.rem(along + j % 4, 4)

    loads = [
        pltpu.make_async_copy(src, dst, load.at[i])
        for i, (src, dst) in enumerate(
            (
                (k_hbm, k_in), (v_hbm, v_in), (tok_hbm, tok), (wq_hbm, w_q),
                (wk_hbm, w_k), (wv_hbm, w_v), (wo_hbm, w_o.at[0]), (fv_hbm, f_v),
                (fg_hbm, f_g), (fd_hbm, f_d),
            )
        )
    ]
    for part in loads:
        part.start()

    barrier = pltpu.get_barrier_semaphore()
    peers = [partner]
    for core in (s, t):
        peers += [dev(y_up, z, core), dev(y_down, z, core)]
        peers += [dev(y, z_up, core), dev(y, z_down, core)]
    peers += [(p, chan_of(j)) for j in range(1, 8)]
    for peer in peers:
        pl.semaphore_signal(barrier, inc=1, device_id=peer, device_id_type=MESH)
    pl.semaphore_wait(barrier, len(peers))

    def split_heads(values):
        first, second = values[:HD], values[HD:]
        mine = jnp.where(s == 0, first, second)
        other = jnp.where(s == 0, second, first)
        return mine, other

    def copy(src, dst, send, recv, peer):
        return pltpu.make_async_remote_copy(
            src_ref=src, dst_ref=dst, send_sem=send, recv_sem=recv,
            device_id=peer, device_id_type=MESH,
        )

    for j, ref in enumerate((k_in, v_in)):
        loads[j].wait()
        mine, other = split_heads(ref[...].T)
        kvb[0, j] = mine
        kvo[0, j] = other
    kv = {
        2: copy(kvb.at[0], kvb.at[2], kv_send.at[2], kv_recv.at[2], dev(y_up, z, s)),
        3: copy(kvo.at[0], kvb.at[3], kv_send.at[3], kv_recv.at[3], dev(y_down, z, t)),
        1: copy(kvo.at[0], kvb.at[1], kv_send.at[1], kv_recv.at[1], partner),
        4: copy(kvo.at[0], kvb.at[4], kv_send.at[4], kv_recv.at[4], dev(y_up, z, t)),
        5: copy(kvb.at[0], kvb.at[5], kv_send.at[5], kv_recv.at[5], dev(y_down, z, s)),
        6: copy(kvb.at[2], kvb.at[6], kv_send.at[6], kv_recv.at[6], dev(y_up, z, s)),
        7: copy(kvb.at[3], kvb.at[7], kv_send.at[7], kv_recv.at[7], dev(y_down, z, s)),
        9: copy(kvo.at[1], kvb.at[9], kv_send.at[9], kv_recv.at[9], partner),
    }
    for j in (2, 3, 1, 4, 5):
        kv[j].start()

    mine_rows = pl.ds(pl.multiple_of(s * HD, HD), HD)
    weights = {}
    for j in range(1, 8):
        weights[j] = copy(
            wo_hbm.at[mine_rows], w_o.at[j, mine_rows], w_send.at[j], w_recv.at[j],
            (p, chan_of(j)),
        )
    passed = {}
    for j in range(1, 8):
        passed[j] = copy(
            w_o.at[j, mine_rows], w_o.at[j, mine_rows], wx_send.at[j], wx_recv.at[j], partner
        )
    for j in (1, 2, 3):
        weights[j].start()

    step = 128
    loads[2].wait()

    def norm_rows(i, _):
        at = pl.ds(pl.multiple_of(i * step, step), step)
        normed[at, :] = normalize(tok[at, :].astype(F32)).astype(BF16)
        return 0

    lax.fori_loop(0, rows // step, norm_rows, 0)

    def project(w):
        return jnp.dot(normed[...], w[...], preferred_element_type=F32).astype(BF16)

    loads[3].wait()
    mine, other = split_heads(project(w_q).T)
    q = {}
    for h in (0, 1):
        qb[0, h] = mine[:, h * half : (h + 1) * half]
        qo[h] = other[:, h * half : (h + 1) * half]
    for h in (0, 1):
        for j, (from_ref, peer) in {
            2: (qb.at[0, h], dev(y, z_up, s)),
            3: (qo.at[h], dev(y, z_down, t)),
            4: (qo.at[h], dev(y, z_up, t)),
            5: (qb.at[0, h], dev(y, z_down, s)),
            1: (qo.at[h], partner),
            6: (qb.at[2, h], dev(y, z_up, s)),
            7: (qb.at[3, h], dev(y, z_down, s)),
        }.items():
            q[j, h] = copy(from_ref, qb.at[j, h], q_send.at[j, h], q_recv.at[j, h], peer)
        for j in (2, 3, 4, 5, 1):
            q[j, h].start()
    for j, w in enumerate((w_k, w_v)):
        loads[4 + j].wait()
        mine, other = split_heads(project(w).T)
        kvb[8, j] = mine
        kvo[1, j] = other
    kv[9].start()

    top[...] = jnp.full(top.shape, LOW, F32)
    total[...] = jnp.zeros(total.shape, F32)
    acc[...] = jnp.zeros(acc.shape, F32)

    def prepare_keys(u):
        key = kvb[u, 0]
        kk[u] = jnp.concatenate([key, key], axis=0).T

    def prepare_queries(f, h):
        scaled = qb[f, h].astype(F32) * SCALE
        high = scaled.astype(BF16)
        low = (scaled - high.astype(F32)).astype(BF16)
        qq[f, h] = jnp.concatenate([high, low], axis=0)

    def score(h, item, s_ref, b_ref):
        f, ua, ub = item
        first = jnp.dot(kk[ua], qq[f, h], preferred_element_type=F32)
        s_ref[:rows] = first
        second = jnp.dot(kk[ub], qq[f, h], preferred_element_type=F32)
        s_ref[rows:] = second
        b_ref[...] = jnp.maximum(
            jnp.max(first, axis=0, keepdims=True), jnp.max(second, axis=0, keepdims=True)
        )

    def absorb(h, item, s_ref, b_ref):
        f, ua, ub = item
        old = top[f, h]
        new = jnp.maximum(old, b_ref[...])
        rescale = jnp.exp2(old - new)
        first = jnp.exp2(s_ref[:rows] - new)
        second = jnp.exp2(s_ref[rows:] - new)
        total[f, h] = (
            total[f, h] * rescale
            + jnp.sum(first, axis=0, keepdims=True)
            + jnp.sum(second, axis=0, keepdims=True)
        )
        acc[f, h] = (
            acc[f, h] * rescale
            + jnp.dot(kvb[ua, 1], first.astype(BF16), preferred_element_type=F32)
            + jnp.dot(kvb[ub, 1], second.astype(BF16), preferred_element_type=F32)
        )
        top[f, h] = new

    def attend(h, count, item):
        score(h, item(0), s_a, b_a)

        def two(i, _):
            first, second = item(2 * i), item(2 * i + 1)
            third = item(jnp.minimum(2 * i + 2, count - 1))
            score(h, second, s_b, b_b)
            absorb(h, first, s_a, b_a)
            score(h, third, s_a, b_a)
            absorb(h, second, s_b, b_b)
            return 0

        lax.fori_loop(0, count // 2, two, 0)

    def block(h, f0, nf, g0, ng):
        def item(i):
            i = jnp.int32(i)
            u = 2 * (g0 + lax.rem(i, ng))
            return f0 + lax.div(i, ng), u, u + 1

        attend(h, nf * ng, item)

    def own_item(i):
        i = jnp.int32(i)
        return i, 8 * (1 - i), 1 + 8 * i

    def keys_ready(*units):
        for u in units:
            kv[u].wait_recv()
            if u in (2, 3):
                kv[u + 4].start()
            prepare_keys(u)

    def queries_ready(h, *units):
        for f in units:
            q[f, h].wait_recv()
            if f in (2, 3):
                q[f + 4, h].start()
            prepare_queries(f, h)

    targets = {
        6: (dev(y, z_up, s), 5),
        7: (dev(y, z_down, s), 6),
        2: (dev(y, z_down, s), 1),
        3: (dev(y, z_up, t), 2),
        4: (dev(y, z_down, t), 3),
        5: (dev(y, z_up, s), 4),
        1: (partner, 0),
    }
    back = {}
    for h in (0, 1):
        for f, (peer, slot) in targets.items():
            back[f, h] = (
                copy(
                    o_out.at[f, h], o_in.at[slot, h], o_send.at[f, h], o_recv.at[slot, h], peer
                ),
                copy(
                    stat_out.at[f, h], stat_in.at[slot, h], t_send.at[f, h],
                    t_recv.at[slot, h], peer,
                ),
            )

    def give(h, *units):
        for f in units:
            o_out[f, h] = acc[f, h].astype(BF16)
            stat_out[f, h, 0:1] = top[f, h]
            stat_out[f, h, 1:2] = total[f, h]
            for part in back[f, h]:
                part.start()

    def arrived(h, *units):
        for f in units:
            for part in back[f, h]:
                part.wait_recv()

    def merge(one, other):
        new = jnp.maximum(one[0], other[0])
        left, right = jnp.exp2(one[0] - new), jnp.exp2(other[0] - new)
        return (
            new,
            one[1] * left + other[1] * right,
            one[2] * left + other[2] * right,
        )

    def received(h, slot):
        return stat_in[slot, h, 0:1], stat_in[slot, h, 1:2], o_in[slot, h].astype(F32)

    def local(h, f):
        return top[f, h], total[f, h], acc[f, h]

    def pass_on(h):
        arrived(h, 6, 7)
        for f, slot in ((5, 5), (4, 6)):
            top[f, h], total[f, h], acc[f, h] = merge(local(h, f), received(h, slot))
        give(h, 4, 5)

    gathers = {}
    for h in (0, 1):
        for j in range(1, 8):
            gathers[j, h] = copy(
                att.at[h, 0], att.at[h, j], a_send.at[j, h], a_recv.at[j, h], (p, chan_of(j))
            )

    def finish(h):
        arrived(h, 1, 2, 3, 4, 5)
        _, sums, values = merge(merge(local(h, 0), received(h, 1)), received(h, 4))
        fin[s] = values / sums
        _, sums, values = merge(merge(received(h, 0), received(h, 2)), received(h, 3))
        fin[t] = values / sums
        att[h, 0] = jnp.concatenate([fin[0], fin[1]], axis=0).T.astype(BF16)
        for j in (5, 7, 4, 1, 3, 6, 2):
            gathers[j, h].start()

    scatters = {}
    for h in (0, 1):
        for j in range(1, 8):
            chunk = pl.ds(pl.multiple_of(chan_of(j) * share, 32), share)
            scatters[j, h] = copy(
                down.at[h, chunk], pieces.at[h, j], r_send.at[j, h], r_recv.at[j, h],
                (p, chan_of(j)),
            )
    my_chunk = pl.ds(pl.multiple_of(c * share, 32), share)

    def feed_forward(h):
        for j in range(1, 8):
            gathers[j, h].wait_recv()
        here = slice(h * half, (h + 1) * half)
        mixed = tok[here].astype(F32)
        for j in range(0, 8, 2):
            mixed += jnp.dot(
                jnp.concatenate([att[h, j], att[h, j + 1]], axis=1),
                w_o[j : j + 2].reshape(4 * HD, w_o.shape[2]),
                preferred_element_type=F32,
            )
        resid[h] = mixed

        def norm_again(i, _):
            at = pl.ds(pl.multiple_of(i * step, step), step)
            normed[at, :] = normalize(resid[h, at, :]).astype(BF16)
            return 0

        lax.fori_loop(0, half // step, norm_again, 0)
        inputs = normed[:half]
        values = jnp.dot(inputs, f_v[...], preferred_element_type=F32)
        gate = jnp.dot(inputs, f_g[...], preferred_element_type=F32)
        gate = 0.5 * gate * (1.0 + lax.erf(gate * math.sqrt(0.5)))
        gated = (values * gate).astype(BF16)
        result = jnp.dot(gated, f_d[...], preferred_element_type=F32)
        down[h] = result.astype(BF16).T
        for j in (5, 7, 4, 1, 3, 6, 2):
            scatters[j, h].start()
        turned[h] = resid[h].T

    def conclude(h):
        sums = turned[h, my_chunk] + down[h, my_chunk].astype(F32)
        for j in range(1, 8):
            scatters[j, h].wait_recv()
            sums += pieces[h, j].astype(F32)
        out[h * half : (h + 1) * half] = sums.T.astype(out.dtype)

    prepare_keys(0)
    prepare_keys(8)
    prepare_queries(0, 0)
    prepare_queries(0, 1)
    keys_ready(1, 9)
    queries_ready(0, 1)
    queries_ready(1, 1)
    attend(0, 2, own_item)
    attend(1, 2, own_item)
    keys_ready(2, 3)
    block(0, 0, 2, 1, 1)
    block(1, 0, 2, 1, 1)
    queries_ready(0, 2, 3)
    keys_ready(4, 5)
    block(0, 2, 2, 0, 3)
    queries_ready(0, 4, 5)
    queries_ready(1, 2, 3)
    block(0, 4, 2, 0, 3)
    queries_ready(0, 6, 7)
    keys_ready(6, 7)
    block(0, 6, 2, 0, 4)
    give(0, 6, 7)
    for j in (4, 5, 6, 7):
        weights[j].start()
    block(0, 2, 4, 3, 1)
    give(0, 2, 3)
    block(0, 0, 2, 2, 2)
    give(0, 1)
    queries_ready(1, 4, 5, 6, 7)
    block(1, 6, 2, 0, 4)
    give(1, 6, 7)
    pass_on(0)
    block(1, 2, 2, 0, 4)
    give(1, 2, 3)
    for j in (1, 2, 3):
        weights[j].wait_recv()
        passed[j].start()
    block(1, 4, 2, 0, 4)
    finish(0)
    pass_on(1)
    block(1, 0, 2, 2, 2)
    give(1, 1)
    for j in (4, 5, 6, 7):
        weights[j].wait_recv()
        passed[j].start()
    for part in loads[6:]:
        part.wait()
    for j in range(1, 8):
        passed[j].wait_recv()
    finish(1)
    feed_forward(0)
    feed_forward(1)
    conclude(0)
    conclude(1)

    for j in (1, 2, 3, 4, 5, 6, 7, 9):
        kv[j].wait_send()
    for j in range(1, 8):
        weights[j].wait_send()
        passed[j].wait_send()
        for h in (0, 1):
            q[j, h].wait_send()
            for part in back[j, h]:
                part.wait_send()
            gathers[j, h].wait_send()
            scatters[j, h].wait_send()


def per_device(
    tokens, stale_k, stale_v, w_query, w_key, w_value, w_out, ff_value, ff_gate, ff_down
):
    _, rows, width = tokens.shape
    half, hidden = rows // 2, ff_value.shape[1]
    share = width // lax.axis_size("chan")
    vmem, dma = pltpu.VMEM, pltpu.SemaphoreType.DMA
    result = pl.pallas_call(
        block_kernel,
        out_shape=jax.ShapeDtypeStruct((rows, share), BF16),
        in_specs=[pl.BlockSpec(memory_space=pl.ANY)] * 10,
        out_specs=pl.BlockSpec(memory_space=vmem),
        scratch_shapes=[
            vmem((rows, width), BF16),
            vmem((rows, 2 * HD), BF16),
            vmem((rows, 2 * HD), BF16),
            vmem((width, 2 * HD), BF16),
            vmem((width, 2 * HD), BF16),
            vmem((width, 2 * HD), BF16),
            vmem((8, 2 * HD, width), BF16),
            vmem((width, hidden), BF16),
            vmem((width, hidden), BF16),
            vmem((hidden, width), BF16),
            vmem((rows, width), BF16),
            vmem((10, 2, HD, rows), BF16),
            vmem((2, 2, HD, rows), BF16),
            vmem((8, 2, HD, half), BF16),
            vmem((2, HD, half), BF16),
            vmem((10, rows, 2 * HD), BF16),
            vmem((8, 2, 2 * HD, half), BF16),
            vmem((2 * rows, half), F32),
            vmem((2 * rows, half), F32),
            vmem((1, half), F32),
            vmem((1, half), F32),
            vmem((8, 2, 1, half), F32),
            vmem((8, 2, 1, half), F32),
            vmem((8, 2, HD, half), F32),
            vmem((8, 2, 2, half), F32),
            vmem((8, 2, HD, half), BF16),
            vmem((7, 2, HD, half), BF16),
            vmem((7, 2, 2, half), F32),
            vmem((2, HD, half), F32),
            vmem((2, 8, half, 2 * HD), BF16),
            vmem((2, half, width), F32),
            vmem((2, width, half), F32),
            vmem((2, width, half), BF16),
            vmem((2, 8, share, half), BF16),
            dma((10,)),
            dma((10,)), dma((10,)), dma((8, 2)), dma((8, 2)),
            dma((8, 2)), dma((7, 2)), dma((8, 2)), dma((7, 2)),
            dma((8,)), dma((8,)), dma((8,)), dma((8,)),
            dma((8, 2)), dma((8, 2)), dma((8, 2)), dma((8, 2)),
        ],
        compiler_params=pltpu.CompilerParams(collective_id=0, has_side_effects=True),
    )(
        tokens[0], stale_k[0], stale_v[0], w_query, w_key, w_value, w_out,
        ff_value, ff_gate, ff_down,
    )
    return result[None]


def solution(mesh):
    return jax.shard_map(
        per_device,
        mesh=mesh,
        in_specs=(
            P(None, "patch", None),
            P(None, "patch", "chan"),
            P(None, "patch", "chan"),
            P(None, "chan"),
            P(None, "chan"),
            P(None, "chan"),
            P("chan", None),
            P(None, "chan"),
            P(None, "chan"),
            P("chan", None),
        ),
        out_specs=P(None, "patch", "chan"),
        check_vma=False,
    )
```

time: 128 us -> 86.3 us (0.67); the launches traced: 126 us -> 86.2 us
  blocking collectives: 39.3 us -> 0 us
  Pallas kernels: 46.2 us -> 84.5 us
  waiting for transfers between devices: 16.5 us -> 0 us
  matrix products: 11.3 us -> 0 us
  starting transfers between devices: 4.69 us -> 0 us
  local copies, waits for them, and re-layouts: 5.51 us -> 1.73 us
  other arithmetic: 2.46 us -> 0 us
    all_to_all x2 -> x0, blocking collectives: 39.3 us -> none  [the longest x1 20.6 us: from_everyone(): return lax.all_to_all(copies, axis, split_axis=0, concat_axis=0, tiled=True)]
    pallas_call x1, Pallas kernels: 46.2 us -> 84.5 us  [per_device(): pl.pallas_call(block_kernel, out_shape=jax.ShapeDtypeStruct((rows, share)...]
    all_to_all x1 -> x0, waiting for transfers between devices: 16.5 us -> none  [sent_and_summed(): lax.all_to_all(split_up(shard, dim, devices), axis, 0, 0, tiled=True)]
    dot_general x3 -> x0, matrix products: 11.3 us -> none  [project(): jnp.einsum('btd,de->bte', inputs, weight, preferred_element_type=jnp.floa...]
    all_to_all x1 -> x0, starting transfers between devices: 4.69 us -> none  [sent_and_summed(): lax.all_to_all(split_up(shard, dim, devices), axis, 0, 0, tiled=True)]
    convert_element_type x2 -> x0, local copies, waits for them, and re-layouts: 3.1 us -> none  [the longest x1 1.6 us: per_device(): ffn_part = sent_and_summed(down_out.astype(jnp.bfloat16), 'chan', 2)]
    broadcast_in_dim x1, local copies, waits for them, and re-layouts: 0.11 us -> 1.73 us  [per_device(): return result[None]]
    convert_element_type x4 -> x0, other arithmetic: 1.5 us -> none  [the longest x1 0.74 us: per_device(): return (resid_share + ffn_part).astype(jnp.bfloat16)]
  transfers between devices with their start and end apart: 1 -> 0, of which waited for: 1 -> 0; matrix products, arithmetic and copies ran while one was open for 1% -> 0% of each run, Pallas kernels for 0% -> 0%
where the time goes in v2:
time: 86.3 us; the launch traced here: 86.2 us
  Pallas kernels  84.5 us (98%)
  local copies, waits for them, and re-layouts  1.73 us (2%)
    pallas_call x1, Pallas kernels, per_device(): pl.pallas_call(block_kernel, out_shape=jax.ShapeDtypeStruct((rows, share)...  84.5 us
    broadcast_in_dim x1, local copies, waits for them, and re-layouts, per_device(): return result[None]  1.73 us

profile of v2, /device:TPU:1, one launch (start us, length us, event | category | flops | bytes accessed | tf_op | source)
XLA Modules:
  0.0 86.2 jit_solution(16864811808542110390)
XLA Ops:
  0.0 84.5 %shard_map.100 = bf16[512,160]{1,0:T(8,128)(2,1)} custom-call(bf16[512,1280]{1,0:T(8,128)(2,1)} %bitcast.4, bf16[512,128]{1,0:T(8,128)(2,1)} %bitcast.6, bf16[512,128]{1,0:T(8,128)(2,1)} %bitcast.7, bf16[1280,128]{1,0:T(8,128)(2,1)} %wq_hbm.1, bf16[1280,128]{1,0:T(8,128)(2,1)} %wk_hbm.1, bf16[1280,128]{1,0:T(8,128)(2,1)} %wv_hbm.1, ...), custom_call_target="tpu_custom_call" | custom-call | tf_op jit(solution)/shard_map/pallas_call | solution.py:440
  84.5 1.7 %copy.11 = bf16[1,512,160]{1,2,0:T(8,128)(2,1)} copy(bf16[1,512,160]{2,1,0:T(8,128)(2,1)} %bitcast.5) | data formatting | bytes 327680 | tf_op jit(solution)/shard_map/broadcast_in_dim | solution.py:491

commit v3 on v2

--- a/solution.py
+++ b/solution.py
@@ -39,6 +39,7 @@
     t = 1 - s
     y_up, y_down = lax.rem(y + 1, 4), lax.rem(y + 3, 4)
     z_up, z_down = lax.rem(z + 1, 4), lax.rem(z + 3, 4)
+    y_far, z_far = lax.rem(y + 2, 4), lax.rem(z + 2, 4)
     across, along = lax.div(c, 4), lax.rem(c, 4)
     rows = tok.shape[0]
     half = rows // 2
@@ -62,7 +63,7 @@
             )
         )
     ]
-    for part in loads:
+    for part in loads[:4]:
         part.start()
 
     barrier = pltpu.get_barrier_semaphore()
@@ -70,10 +71,10 @@
     for core in (s, t):
         peers += [dev(y_up, z, core), dev(y_down, z, core)]
         peers += [dev(y, z_up, core), dev(y, z_down, core)]
+        peers += [dev(y_far, z, core), dev(y, z_far, core)]
     peers += [(p, chan_of(j)) for j in range(1, 8)]
     for peer in peers:
         pl.semaphore_signal(barrier, inc=1, device_id=peer, device_id_type=MESH)
-    pl.semaphore_wait(barrier, len(peers))
 
     def split_heads(values):
         first, second = values[:HD], values[HD:]
@@ -92,32 +93,36 @@
         mine, other = split_heads(ref[...].T)
         kvb[0, j] = mine
         kvo[0, j] = other
+    pl.semaphore_wait(barrier, len(peers))
     kv = {
         2: copy(kvb.at[0], kvb.at[2], kv_send.at[2], kv_recv.at[2], dev(y_up, z, s)),
         3: copy(kvo.at[0], kvb.at[3], kv_send.at[3], kv_recv.at[3], dev(y_down, z, t)),
         1: copy(kvo.at[0], kvb.at[1], kv_send.at[1], kv_recv.at[1], partner),
         4: copy(kvo.at[0], kvb.at[4], kv_send.at[4], kv_recv.at[4], dev(y_up, z, t)),
         5: copy(kvb.at[0], kvb.at[5], kv_send.at[5], kv_recv.at[5], dev(y_down, z, s)),
-        6: copy(kvb.at[2], kvb.at[6], kv_send.at[6], kv_recv.at[6], dev(y_up, z, s)),
-        7: copy(kvb.at[3], kvb.at[7], kv_send.at[7], kv_recv.at[7], dev(y_down, z, s)),
+        6: copy(kvb.at[0], kvb.at[6], kv_send.at[6], kv_recv.at[6], dev(y_far, z, s)),
+        7: copy(kvo.at[0], kvb.at[7], kv_send.at[7], kv_recv.at[7], dev(y_far, z, t)),
         9: copy(kvo.at[1], kvb.at[9], kv_send.at[9], kv_recv.at[9], partner),
     }
-    for j in (2, 3, 1, 4, 5):
+    for j in (2, 3, 1, 4, 5, 6, 7):
         kv[j].start()
 
     mine_rows = pl.ds(pl.multiple_of(s * HD, HD), HD)
     weights = {}
     for j in range(1, 8):
         weights[j] = copy(
-            wo_hbm.at[mine_rows], w_o.at[j, mine_rows], w_send.at[j], w_recv.at[j],
-            (p, chan_of(j)),
+            wo_hbm.at[mine_rows] if j < 5 else w_o.at[4, mine_rows],
+            w_o.at[j, mine_rows], w_send.at[j], w_recv.at[j],
+            (p, chan_of(j if j < 5 else j - 4)),
         )
     passed = {}
     for j in range(1, 8):
         passed[j] = copy(
             w_o.at[j, mine_rows], w_o.at[j, mine_rows], wx_send.at[j], wx_recv.at[j], partner
         )
-    for j in (1, 2, 3):
+    for part in loads[4:]:
+        part.start()
+    for j in (1, 3, 2):
         weights[j].start()
 
     step = 128
@@ -128,17 +133,12 @@
         normed[at, :] = normalize(tok[at, :].astype(F32)).astype(BF16)
         return 0
 
-    lax.fori_loop(0, rows // step, norm_rows, 0)
-
-    def project(w):
-        return jnp.dot(normed[...], w[...], preferred_element_type=F32).astype(BF16)
+    def project(w, here):
+        result = jnp.dot(normed[here], w[...], preferred_element_type=F32)
+        return split_heads(result.astype(BF16).T)
 
     loads[3].wait()
-    mine, other = split_heads(project(w_q).T)
     q = {}
-    for h in (0, 1):
-        qb[0, h] = mine[:, h * half : (h + 1) * half]
-        qo[h] = other[:, h * half : (h + 1) * half]
     for h in (0, 1):
         for j, (from_ref, peer) in {
             2: (qb.at[0, h], dev(y, z_up, s)),
@@ -146,17 +146,19 @@
             4: (qo.at[h], dev(y, z_up, t)),
             5: (qb.at[0, h], dev(y, z_down, s)),
             1: (qo.at[h], partner),
-            6: (qb.at[2, h], dev(y, z_up, s)),
-            7: (qb.at[3, h], dev(y, z_down, s)),
+            6: (qb.at[0, h], dev(y, z_far, s)),
+            7: (qo.at[h], dev(y, z_far, t)),
         }.items():
             q[j, h] = copy(from_ref, qb.at[j, h], q_send.at[j, h], q_recv.at[j, h], peer)
-        for j in (2, 3, 4, 5, 1):
+    for h in (0, 1):
+        lax.fori_loop(h * half // step, (h + 1) * half // step, norm_rows, 0)
+        qb[0, h], qo[h] = project(w_q, slice(h * half, (h + 1) * half))
+        for j in (1, 2, 3, 4, 5, 6, 7):
             q[j, h].start()
+    weights[4].start()
     for j, w in enumerate((w_k, w_v)):
         loads[4 + j].wait()
-        mine, other = split_heads(project(w).T)
-        kvb[8, j] = mine
-        kvo[1, j] = other
+        kvb[8, j], kvo[1, j] = project(w, slice(0, rows))
     kv[9].start()
 
     top[...] = jnp.full(top.shape, LOW, F32)
@@ -231,20 +233,16 @@
     def keys_ready(*units):
         for u in units:
             kv[u].wait_recv()
-            if u in (2, 3):
-                kv[u + 4].start()
             prepare_keys(u)
 
     def queries_ready(h, *units):
         for f in units:
             q[f, h].wait_recv()
-            if f in (2, 3):
-                q[f + 4, h].start()
             prepare_queries(f, h)
 
     targets = {
-        6: (dev(y, z_up, s), 5),
-        7: (dev(y, z_down, s), 6),
+        6: (dev(y, z_far, s), 5),
+        7: (dev(y, z_far, t), 6),
         2: (dev(y, z_down, s), 1),
         3: (dev(y, z_up, t), 2),
         4: (dev(y, z_down, t), 3),
@@ -292,27 +290,25 @@
     def local(h, f):
         return top[f, h], total[f, h], acc[f, h]
 
-    def pass_on(h):
-        arrived(h, 6, 7)
-        for f, slot in ((5, 5), (4, 6)):
-            top[f, h], total[f, h], acc[f, h] = merge(local(h, f), received(h, slot))
-        give(h, 4, 5)
-
     gathers = {}
     for h in (0, 1):
         for j in range(1, 8):
+            relay = h == 0 and j > 4
             gathers[j, h] = copy(
-                att.at[h, 0], att.at[h, j], a_send.at[j, h], a_recv.at[j, h], (p, chan_of(j))
+                att.at[h, 4 if relay else 0], att.at[h, j], a_send.at[j, h], a_recv.at[j, h],
+                (p, chan_of(j - 4 if relay else j)),
             )
 
     def finish(h):
-        arrived(h, 1, 2, 3, 4, 5)
-        _, sums, values = merge(merge(local(h, 0), received(h, 1)), received(h, 4))
-        fin[s] = values / sums
-        _, sums, values = merge(merge(received(h, 0), received(h, 2)), received(h, 3))
-        fin[t] = values / sums
+        arrived(h, 1, 2, 3, 4, 5, 6, 7)
+        for head, parts in (
+            (s, (local(h, 0), received(h, 1), received(h, 4), received(h, 5))),
+            (t, (received(h, 0), received(h, 2), received(h, 3), received(h, 6))),
+        ):
+            _, sums, values = functools.reduce(merge, parts)
+            fin[head] = values / sums
         att[h, 0] = jnp.concatenate([fin[0], fin[1]], axis=0).T.astype(BF16)
-        for j in (5, 7, 4, 1, 3, 6, 2):
+        for j in (4, 1, 3, 2) if h == 0 else (5, 7, 4, 1, 3, 6, 2):
             gathers[j, h].start()
 
     scatters = {}
@@ -327,7 +323,8 @@
 
     def feed_forward(h):
         for j in range(1, 8):
-            gathers[j, h].wait_recv()
+            if h == 1 or j != 4:
+                gathers[j, h].wait_recv()
         here = slice(h * half, (h + 1) * half)
         mixed = tok[here].astype(F32)
         for j in range(0, 8, 2):
@@ -378,33 +375,35 @@
     keys_ready(4, 5)
     block(0, 2, 2, 0, 3)
     queries_ready(0, 4, 5)
-    queries_ready(1, 2, 3)
     block(0, 4, 2, 0, 3)
     queries_ready(0, 6, 7)
     keys_ready(6, 7)
     block(0, 6, 2, 0, 4)
     give(0, 6, 7)
-    for j in (4, 5, 6, 7):
-        weights[j].start()
     block(0, 2, 4, 3, 1)
-    give(0, 2, 3)
+    give(0, 2, 3, 4, 5)
     block(0, 0, 2, 2, 2)
     give(0, 1)
-    queries_ready(1, 4, 5, 6, 7)
+    weights[4].wait_recv()
+    for j in (5, 7, 6):
+        weights[j].start()
+    queries_ready(1, 2, 3, 4, 5, 6, 7)
     block(1, 6, 2, 0, 4)
     give(1, 6, 7)
-    pass_on(0)
+    for j in (1, 2, 3):
+        weights[j].wait_recv()
+    for j in (1, 2, 3, 4):
+        passed[j].start()
     block(1, 2, 2, 0, 4)
     give(1, 2, 3)
-    for j in (1, 2, 3):
-        weights[j].wait_recv()
-        passed[j].start()
+    finish(0)
     block(1, 4, 2, 0, 4)
-    finish(0)
-    pass_on(1)
+    give(1, 4, 5)
     block(1, 0, 2, 2, 2)
     give(1, 1)
-    for j in (4, 5, 6, 7):
+    gathers[4, 0].wait_recv()
+    for j in (5, 7, 6):
+        gathers[j, 0].start()
         weights[j].wait_recv()
         passed[j].start()
     for part in loads[6:]:

time: 86.3 us -> 72.4 us (0.84)
  Pallas kernels: 84.5 us -> 70.5 us
    pallas_call x1, Pallas kernels: 84.5 us -> 70.5 us  [per_device(): pl.pallas_call(block_kernel, out_shape=jax.ShapeDtypeStruct((rows, share)...]
where the time goes in v3:
time: 72.4 us; the launch traced here: 72.3 us
  Pallas kernels  70.5 us (97%)
  local copies, waits for them, and re-layouts  1.73 us (2%)
    pallas_call x1, Pallas kernels, per_device(): pl.pallas_call(block_kernel, out_shape=jax.ShapeDtypeStruct((rows, share)...  70.5 us
    broadcast_in_dim x1, local copies, waits for them, and re-layouts, per_device(): return result[None]  1.73 us

profile of v3, /device:TPU:1, one launch (start us, length us, event | category | flops | bytes accessed | tf_op | source)
XLA Modules:
  0.0 72.3 jit_solution(7668949705161572353)
XLA Ops:
  0.0 70.5 %shard_map.100 = bf16[512,160]{1,0:T(8,128)(2,1)} custom-call(bf16[512,1280]{1,0:T(8,128)(2,1)} %bitcast.4, bf16[512,128]{1,0:T(8,128)(2,1)} %bitcast.6, bf16[512,128]{1,0:T(8,128)(2,1)} %bitcast.7, bf16[1280,128]{1,0:T(8,128)(2,1)} %wq_hbm.1, bf16[1280,128]{1,0:T(8,128)(2,1)} %wk_hbm.1, bf16[1280,128]{1,0:T(8,128)(2,1)} %wv_hbm.1, ...), custom_call_target="tpu_custom_call" | custom-call | tf_op jit(solution)/shard_map/pallas_call | solution.py:439
  70.5 1.7 %copy.11 = bf16[1,512,160]{1,2,0:T(8,128)(2,1)} copy(bf16[1,512,160]{2,1,0:T(8,128)(2,1)} %bitcast.5) | data formatting | bytes 327680 | tf_op jit(solution)/shard_map/broadcast_in_dim | solution.py:490

commit v4 on v3

--- a/solution.py
+++ b/solution.py
@@ -25,7 +25,7 @@
 
 def block_kernel(
     tok_hbm, k_hbm, v_hbm, wq_hbm, wk_hbm, wv_hbm, wo_hbm, fv_hbm, fg_hbm, fd_hbm, out,
-    tok, k_in, v_in, w_q, w_k, w_v, w_o, f_v, f_g, f_d,
+    tok, k_in, v_in, w_q, w_kv, w_o, f_vg, f_d,
     normed, kvb, kvo, qb, qo, kk, qq, s_a, s_b, b_a, b_b,
     top, total, acc, stat_out, o_out, o_in, stat_in, fin,
     att, resid, turned, down, pieces,
@@ -43,7 +43,8 @@
     across, along = lax.div(c, 4), lax.rem(c, 4)
     rows = tok.shape[0]
     half = rows // 2
-    share = out.shape[1]
+    share = out.shape[0]
+    hidden = f_d.shape[0]
 
     def dev(y, z, s):
         return ((y * 4 + z) * 2 + s, c)
@@ -58,8 +59,8 @@
         for i, (src, dst) in enumerate(
             (
                 (k_hbm, k_in), (v_hbm, v_in), (tok_hbm, tok), (wq_hbm, w_q),
-                (wk_hbm, w_k), (wv_hbm, w_v), (wo_hbm, w_o.at[0]), (fv_hbm, f_v),
-                (fg_hbm, f_g), (fd_hbm, f_d),
+                (wk_hbm, w_kv.at[:, : 2 * HD]), (wv_hbm, w_kv.at[:, 2 * HD :]), (wo_hbm, w_o.at[0]),
+                (fv_hbm, f_vg.at[:, :hidden]), (fg_hbm, f_vg.at[:, hidden:]), (fd_hbm, f_d),
             )
         )
     ]
@@ -135,7 +136,7 @@
 
     def project(w, here):
         result = jnp.dot(normed[here], w[...], preferred_element_type=F32)
-        return split_heads(result.astype(BF16).T)
+        return result.astype(BF16).T
 
     loads[3].wait()
     q = {}
@@ -152,13 +153,16 @@
             q[j, h] = copy(from_ref, qb.at[j, h], q_send.at[j, h], q_recv.at[j, h], peer)
     for h in (0, 1):
         lax.fori_loop(h * half // step, (h + 1) * half // step, norm_rows, 0)
-        qb[0, h], qo[h] = project(w_q, slice(h * half, (h + 1) * half))
+        qb[0, h], qo[h] = split_heads(project(w_q, slice(h * half, (h + 1) * half)))
         for j in (1, 2, 3, 4, 5, 6, 7):
             q[j, h].start()
-    weights[4].start()
-    for j, w in enumerate((w_k, w_v)):
-        loads[4 + j].wait()
-        kvb[8, j], kvo[1, j] = project(w, slice(0, rows))
+        if h == 0:
+            weights[4].start()
+    loads[4].wait()
+    loads[5].wait()
+    both = project(w_kv, slice(0, rows))
+    for j in (0, 1):
+        kvb[8, j], kvo[1, j] = split_heads(both[j * 2 * HD : (j + 1) * 2 * HD])
     kv[9].start()
 
     top[...] = jnp.full(top.shape, LOW, F32)
@@ -175,60 +179,62 @@
         low = (scaled - high.astype(F32)).astype(BF16)
         qq[f, h] = jnp.concatenate([high, low], axis=0)
 
-    def score(h, item, s_ref, b_ref):
-        f, ua, ub = item
-        first = jnp.dot(kk[ua], qq[f, h], preferred_element_type=F32)
-        s_ref[:rows] = first
-        second = jnp.dot(kk[ub], qq[f, h], preferred_element_type=F32)
-        s_ref[rows:] = second
-        b_ref[...] = jnp.maximum(
-            jnp.max(first, axis=0, keepdims=True), jnp.max(second, axis=0, keepdims=True)
-        )
-
-    def absorb(h, item, s_ref, b_ref):
-        f, ua, ub = item
-        old = top[f, h]
-        new = jnp.maximum(old, b_ref[...])
-        rescale = jnp.exp2(old - new)
-        first = jnp.exp2(s_ref[:rows] - new)
-        second = jnp.exp2(s_ref[rows:] - new)
-        total[f, h] = (
-            total[f, h] * rescale
-            + jnp.sum(first, axis=0, keepdims=True)
-            + jnp.sum(second, axis=0, keepdims=True)
-        )
-        acc[f, h] = (
-            acc[f, h] * rescale
-            + jnp.dot(kvb[ua, 1], first.astype(BF16), preferred_element_type=F32)
-            + jnp.dot(kvb[ub, 1], second.astype(BF16), preferred_element_type=F32)
-        )
-        top[f, h] = new
-
-    def attend(h, count, item):
-        score(h, item(0), s_a, b_a)
+    def score(item, s_ref, b_ref):
+        h, pair, *units = item
+        for side, u in enumerate(units):
+            values = jnp.dot(kk[u], qq[2 * pair + side, h], preferred_element_type=F32)
+            s_ref[side] = values
+            b_ref[side] = jnp.max(values, axis=0, keepdims=True)
+
+    def absorb(item, s_ref, b_ref):
+        h, pair, *units = item
+        for side, u in enumerate(units):
+            f = 2 * pair + side
+            old = top[f, h]
+            new = jnp.maximum(old, b_ref[side])
+            rescale = jnp.exp2(old - new)
+            weights = jnp.exp2(s_ref[side] - new)
+            total[f, h] = total[f, h] * rescale + jnp.sum(weights, axis=0, keepdims=True)
+            acc[f, h] = acc[f, h] * rescale + jnp.dot(
+                kvb[u, 1], weights.astype(BF16), preferred_element_type=F32
+            )
+            top[f, h] = new
+
+    def block(h, first_pair, pairs, first_unit, units):
+        def item(i):
+            i = jnp.int32(i)
+            u = first_unit + lax.rem(i, units)
+            return jnp.int32(h), first_pair + lax.div(i, units), u, u
+
+        return pairs * units, item
+
+    def own_block(h):
+        def item(i):
+            i = jnp.int32(i)
+            return jnp.int32(h), jnp.int32(0), 8 - 7 * i, 9 * i
+
+        return 2, item
+
+    def attend(this, then=None, started=False):
+        count, item = this
+        if not started:
+            score(item(0), s_a, b_a)
+        following = item(count - 1) if then is None else then[1](0)
 
         def two(i, _):
             first, second = item(2 * i), item(2 * i + 1)
-            third = item(jnp.minimum(2 * i + 2, count - 1))
-            score(h, second, s_b, b_b)
-            absorb(h, first, s_a, b_a)
-            score(h, third, s_a, b_a)
-            absorb(h, second, s_b, b_b)
+            more = 2 * i + 2 < count
+            third = tuple(
+                jnp.where(more, inner, after)
+                for inner, after in zip(item(2 * i + 2), following)
+            )
+            score(second, s_b, b_b)
+            absorb(first, s_a, b_a)
+            score(third, s_a, b_a)
+            absorb(second, s_b, b_b)
             return 0
 
         lax.fori_loop(0, count // 2, two, 0)
-
-    def block(h, f0, nf, g0, ng):
-        def item(i):
-            i = jnp.int32(i)
-            u = 2 * (g0 + lax.rem(i, ng))
-            return f0 + lax.div(i, ng), u, u + 1
-
-        attend(h, nf * ng, item)
-
-    def own_item(i):
-        i = jnp.int32(i)
-        return i, 8 * (1 - i), 1 + 8 * i
 
     def keys_ready(*units):
         for u in units:
@@ -342,22 +348,22 @@
 
         lax.fori_loop(0, half // step, norm_again, 0)
         inputs = normed[:half]
-        values = jnp.dot(inputs, f_v[...], preferred_element_type=F32)
-        gate = jnp.dot(inputs, f_g[...], preferred_element_type=F32)
+        both = jnp.dot(inputs, f_vg[...], preferred_element_type=F32)
+        values, gate = both[:, :hidden], both[:, hidden:]
         gate = 0.5 * gate * (1.0 + lax.erf(gate * math.sqrt(0.5)))
         gated = (values * gate).astype(BF16)
         result = jnp.dot(gated, f_d[...], preferred_element_type=F32)
         down[h] = result.astype(BF16).T
         for j in (5, 7, 4, 1, 3, 6, 2):
             scatters[j, h].start()
+
+    def conclude(h):
         turned[h] = resid[h].T
-
-    def conclude(h):
         sums = turned[h, my_chunk] + down[h, my_chunk].astype(F32)
         for j in range(1, 8):
             scatters[j, h].wait_recv()
             sums += pieces[h, j].astype(F32)
-        out[h * half : (h + 1) * half] = sums.T.astype(out.dtype)
+        out[:, h * half : (h + 1) * half] = sums.astype(out.dtype)
 
     prepare_keys(0)
     prepare_keys(8)
@@ -366,51 +372,59 @@
     keys_ready(1, 9)
     queries_ready(0, 1)
     queries_ready(1, 1)
-    attend(0, 2, own_item)
-    attend(1, 2, own_item)
+    attend(own_block(0), own_block(1))
+    attend(own_block(1), started=True)
     keys_ready(2, 3)
-    block(0, 0, 2, 1, 1)
-    block(1, 0, 2, 1, 1)
+    attend(block(0, 0, 1, 2, 2), block(1, 0, 1, 2, 2))
+    attend(block(1, 0, 1, 2, 2), started=True)
     queries_ready(0, 2, 3)
+    attend(block(0, 1, 1, 0, 4))
     keys_ready(4, 5)
-    block(0, 2, 2, 0, 3)
     queries_ready(0, 4, 5)
-    block(0, 4, 2, 0, 3)
+    attend(block(0, 1, 1, 4, 2), block(0, 2, 1, 0, 6))
+    attend(block(0, 2, 1, 0, 6), started=True)
     queries_ready(0, 6, 7)
     keys_ready(6, 7)
-    block(0, 6, 2, 0, 4)
+    ahead = [
+        block(0, 1, 1, 6, 2), block(0, 2, 1, 6, 2), block(0, 3, 1, 0, 8), block(0, 0, 1, 4, 4),
+        block(1, 3, 1, 0, 8), block(1, 1, 1, 0, 8), block(1, 2, 1, 0, 8), block(1, 0, 1, 4, 4),
+    ]
+    attend(ahead[0], ahead[1])
+    give(0, 2, 3)
+    attend(ahead[1], ahead[2], started=True)
+    give(0, 4, 5)
+    attend(ahead[2], ahead[3], started=True)
     give(0, 6, 7)
-    block(0, 2, 4, 3, 1)
-    give(0, 2, 3, 4, 5)
-    block(0, 0, 2, 2, 2)
+    attend(ahead[3], started=True)
     give(0, 1)
     weights[4].wait_recv()
     for j in (5, 7, 6):
         weights[j].start()
     queries_ready(1, 2, 3, 4, 5, 6, 7)
-    block(1, 6, 2, 0, 4)
+    attend(ahead[4], ahead[5])
     give(1, 6, 7)
     for j in (1, 2, 3):
         weights[j].wait_recv()
     for j in (1, 2, 3, 4):
         passed[j].start()
-    block(1, 2, 2, 0, 4)
+    attend(ahead[5], ahead[6], started=True)
     give(1, 2, 3)
     finish(0)
-    block(1, 4, 2, 0, 4)
+    attend(ahead[6], ahead[7], started=True)
     give(1, 4, 5)
-    block(1, 0, 2, 2, 2)
+    attend(ahead[7], started=True)
     give(1, 1)
     gathers[4, 0].wait_recv()
     for j in (5, 7, 6):
         gathers[j, 0].start()
+    for j in (5, 7, 6):
         weights[j].wait_recv()
         passed[j].start()
+    finish(1)
     for part in loads[6:]:
         part.wait()
     for j in range(1, 8):
         passed[j].wait_recv()
-    finish(1)
     feed_forward(0)
     feed_forward(1)
     conclude(0)
@@ -438,7 +452,7 @@
     vmem, dma = pltpu.VMEM, pltpu.SemaphoreType.DMA
     result = pl.pallas_call(
         block_kernel,
-        out_shape=jax.ShapeDtypeStruct((rows, share), BF16),
+        out_shape=jax.ShapeDtypeStruct((share, rows), BF16),
         in_specs=[pl.BlockSpec(memory_space=pl.ANY)] * 10,
         out_specs=pl.BlockSpec(memory_space=vmem),
         scratch_shapes=[
@@ -446,11 +460,9 @@
             vmem((rows, 2 * HD), BF16),
             vmem((rows, 2 * HD), BF16),
             vmem((width, 2 * HD), BF16),
-            vmem((width, 2 * HD), BF16),
-            vmem((width, 2 * HD), BF16),
+            vmem((width, 4 * HD), BF16),
             vmem((8, 2 * HD, width), BF16),
-            vmem((width, hidden), BF16),
-            vmem((width, hidden), BF16),
+            vmem((width, 2 * hidden), BF16),
             vmem((hidden, width), BF16),
             vmem((rows, width), BF16),
             vmem((10, 2, HD, rows), BF16),
@@ -459,10 +471,10 @@
             vmem((2, HD, half), BF16),
             vmem((10, rows, 2 * HD), BF16),
             vmem((8, 2, 2 * HD, half), BF16),
-            vmem((2 * rows, half), F32),
-            vmem((2 * rows, half), F32),
-            vmem((1, half), F32),
-            vmem((1, half), F32),
+            vmem((2, rows, half), F32),
+            vmem((2, rows, half), F32),
+            vmem((2, 1, half), F32),
+            vmem((2, 1, half), F32),
             vmem((8, 2, 1, half), F32),
             vmem((8, 2, 1, half), F32),
             vmem((8, 2, HD, half), F32),
@@ -487,7 +499,7 @@
         tokens[0], stale_k[0], stale_v[0], w_query, w_key, w_value, w_out,
         ff_value, ff_gate, ff_down,
     )
-    return result[None]
+    return result.T[None]
 
 
 def solution(mesh):

time: 72.4 us -> 71.8 us (level); the launches traced: 72.3 us -> 70.9 us
  Pallas kernels: 70.5 us -> 69.3 us
    broadcast_in_dim x1 -> x0, local copies, waits for them, and re-layouts: 1.73 us -> none  [per_device(): return result[None]]
    unnamed x0 -> x1, local copies, waits for them, and re-layouts: none -> 1.59 us
    pallas_call x1, Pallas kernels: 70.5 us -> 69.3 us  [per_device(): pl.pallas_call(block_kernel, out_shape=jax.ShapeDtypeStruct((share, rows)...]
where the time goes in v4:
time: 71.8 us; the launch traced here: 70.9 us
  Pallas kernels  69.3 us (97%)
  local copies, waits for them, and re-layouts  1.59 us (2%)
    pallas_call x1, Pallas kernels, per_device(): pl.pallas_call(block_kernel, out_shape=jax.ShapeDtypeStruct((share, rows)...  69.3 us
    unnamed x1, local copies, waits for them, and re-layouts  1.59 us

profile of v4, /device:TPU:1, one launch (start us, length us, event | category | flops | bytes accessed | tf_op | source)
XLA Modules:
  0.0 70.9 jit_solution(11564717858018743000)
XLA Ops:
  0.0 69.3 %shard_map.100 = bf16[160,512]{1,0:T(8,128)(2,1)} custom-call(bf16[512,1280]{1,0:T(8,128)(2,1)} %bitcast.6, bf16[512,128]{1,0:T(8,128)(2,1)} %bitcast.8, bf16[512,128]{1,0:T(8,128)(2,1)} %bitcast.9, bf16[1280,128]{1,0:T(8,128)(2,1)} %wq_hbm.1, bf16[1280,128]{1,0:T(8,128)(2,1)} %wk_hbm.1, bf16[1280,128]{1,0:T(8,128)(2,1)} %wv_hbm.1, ...), custom_call_target="tpu_custom_call" | custom-call | tf_op jit(solution)/shard_map/pallas_call | solution.py:453
  69.3 1.6 %copy.12 = bf16[1,512,160]{1,2,0:T(8,128)(2,1)} copy(bf16[1,512,160]{1,2,0:T(8,128)(2,1)} %bitcast.7) | data formatting | bytes 327680
